TPU v7x, 32 devices: a whole 2x2x4 slice. The times are simulated.
32 devices in a mesh: blk: 8 (over z, y), dp: 4 (over x, core).
Axes of the slice: x: 2, y: 2, z: 4, core: 2. Of those that a mesh axis runs over, the one named last changes fastest.
Arguments:
- memory: float32 [65536, 172], P(('blk', 'dp')), may hold values from -3 to 3
- src: int32 [2, 4096], P(None, ('blk', 'dp')), may hold values from 0 to 2047, as said below
- dst: int32 [2, 4096], P(None, ('blk', 'dp')), may hold values from 0 to 2047, as said below
- negative: int32 [2, 4096], P(None, ('blk', 'dp')), may hold values from 0 to 2047
- event_time: int32 [2, 4096], P(None, ('blk', 'dp')), may hold values from 0 to 1023
- neighbours: int32 [2, 10, 12288], P(None, None, ('blk', 'dp')), may hold values from 0 to 2047
- neighbour_time: int32 [2, 10, 12288], P(None, None, ('blk', 'dp')), may hold values from 0 to 1023
- time_omega: float32 [100], replicated, may hold values from 0.001 to 1
- w_input: float32 [444, 516], replicated, may hold values from -0.25 to 0.25
- w_hidden: float32 [172, 516], replicated, may hold values from -0.4375 to 0.4375
- gru_bias: float32 [2, 516], replicated, may hold values from -3 to 3
- w_query: float32 [172, 172], replicated, may hold values from -0.4807515 to 0.4807515
- w_keyval: float32 [272, 344], replicated, may hold values from -0.7508627 to 0.7508627
- w_decode: float32 [172], replicated, may hold values from -0.875 to 0.875
Outputs:
- memory_out: float32 [65536, 172], P(('blk', 'dp'))
- losses: float32 [2], replicated
- w_input_out: float32 [444, 516], replicated
- w_hidden_out: float32 [172, 516], replicated
- gru_bias_out: float32 [2, 516], replicated
- w_query_out: float32 [172, 172], replicated
- w_keyval_out: float32 [272, 344], replicated
- w_decode_out: float32 [172], replicated
Inputs may be any that keep to these rules, and one draw needn't show every extreme that they name: In each step and event block, the 128 src and 128 dst entries are 256 different rows. `dst`: different from every src entry of the same step and event block, and from each other.
All inputs are finite; a program needn't handle non-finite values.
Results may differ from a plain program's by a relative error of at most 0.00012.
Values sent between devices are 32-bit elements; how exact they have to be, the bound alone decides.
No kernel may reach another device: no remote copies, remote signals or barrier semaphores. Data moves between devices by JAX's collectives and lax.ppermute only.
A program may use at most 128 MiB of HBM per device.

v0:
```python
import jax
import jax.numpy as jnp
from jax import lax
from jax.sharding import PartitionSpec as P

HEADS = 2
STEPS = 2


rate = 0.25
exact = lax.Precision.HIGHEST


def passed_along(shard, axis, by):
    devices = lax.axis_size(axis)
    return lax.ppermute(shard, axis, [(i, (i + by) % devices) for i in range(devices)])


def step_loss(params, memory, src_ids, dst_ids, neg_ids, times, nbr_ids, nbr_times, omega, count):
    w_input, w_hidden, gru_bias, w_query, w_keyval, w_decode = params
    width = memory.shape[1]
    events = src_ids.shape[0]
    h_src = memory[src_ids]
    h_dst = memory[dst_ids]
    stamp = times.astype(jnp.float32)
    tenc = jnp.cos(stamp[:, None] * omega[None, :])
    inputs = jnp.concatenate(
        [jnp.concatenate([h_src, h_dst, tenc], 1), jnp.concatenate([h_dst, h_src, tenc], 1)], 0
    )
    hidden = jnp.concatenate([h_src, h_dst], 0)
    gate_in = (
        jnp.dot(inputs, w_input, precision=exact, preferred_element_type=jnp.float32) + gru_bias[0]
    )
    gate_hid = (
        jnp.dot(hidden, w_hidden, precision=exact, preferred_element_type=jnp.float32) + gru_bias[1]
    )
    reset = jax.nn.sigmoid(gate_in[:, :width] + gate_hid[:, :width])
    update = jax.nn.sigmoid(gate_in[:, width : 2 * width] + gate_hid[:, width : 2 * width])
    cand = jnp.tanh(gate_in[:, 2 * width :] + reset * gate_hid[:, 2 * width :])
    fresh = (1.0 - update) * cand + update * hidden
    touched = jnp.concatenate([src_ids, dst_ids], 0)
    updated = memory.at[touched].set(fresh)
    query_ids = jnp.concatenate([src_ids, dst_ids, neg_ids], 0)
    query_mem = updated[query_ids]
    rows = query_ids.shape[0]
    row_time = jnp.concatenate([stamp, stamp, stamp], 0)
    nbr_mem = updated[nbr_ids]
    delta = row_time[None, :] - nbr_times.astype(jnp.float32)
    nenc = jnp.cos(delta[:, :, None] * omega[None, None, :])
    key_in = jnp.concatenate([nbr_mem, nenc], 2)
    count_nbr = key_in.shape[0]
    keyval = jnp.dot(
        key_in.reshape(count_nbr * rows, -1),
        w_keyval,
        precision=exact,
        preferred_element_type=jnp.float32,
    )
    keyval = keyval.reshape(count_nbr, rows, 2 * width)
    query = jnp.dot(query_mem, w_query, precision=exact, preferred_element_type=jnp.float32)
    head_size = width // HEADS
    keys = keyval[:, :, :width].reshape(count_nbr, rows, HEADS, head_size)
    values = keyval[:, :, width:].reshape(count_nbr, rows, HEADS, head_size)
    query = query.reshape(rows, HEADS, head_size)
    scores = jnp.sum(keys * query[None], -1) / jnp.sqrt(jnp.float32(head_size))
    top = jnp.max(scores, 0, keepdims=True)
    probs = jnp.exp(scores - top)
    probs = probs / jnp.sum(probs, 0, keepdims=True)
    attn = jnp.sum(probs[:, :, :, None] * values, 0).reshape(rows, width)
    embed = query_mem + attn
    e_src = embed[:events]
    e_dst = embed[events : 2 * events]
    e_neg = embed[2 * events :]
    pos = jnp.sum(e_src * e_dst * w_decode[None, :], 1)
    neg = jnp.sum(e_src * e_neg * w_decode[None, :], 1)
    loss = jnp.sum(jax.nn.softplus(-pos) + jax.nn.softplus(neg)) / count
    return (loss, (updated, fresh))


def summed_terms(grads, loss):
    result = lax.psum(tuple(grads) + (loss,), ("blk", "dp"))
    return (tuple(result[:-1]), result[-1])


def on_device(
    memory,
    src,
    dst,
    negative,
    event_time,
    neighbours,
    neighbour_time,
    time_omega,
    w_input,
    w_hidden,
    gru_bias,
    w_query,
    w_keyval,
    w_decode,
):
    params = (w_input, w_hidden, gru_bias, w_query, w_keyval, w_decode)
    count = jnp.float32(src.shape[1] * lax.axis_size("blk") * lax.axis_size("dp"))
    losses = []
    for step in range(STEPS):
        current = memory
        fn = lambda p: step_loss(
            p,
            current,
            src[step],
            dst[step],
            negative[step],
            event_time[step],
            neighbours[step],
            neighbour_time[step],
            time_omega,
            count,
        )
        loss, back, extra = jax.vjp(fn, params, has_aux=True)
        updated, fresh = extra
        grads = back(jnp.float32(1.0))[0]
        sums, total = summed_terms(grads, loss)
        params = tuple((p - rate * g for p, g in zip(params, sums)))
        losses.append(total)
        memory = passed_along(updated, "blk", 1)
    return (
        memory,
        jnp.stack(losses),
        params[0],
        params[1],
        params[2],
        params[3],
        params[4],
        params[5],
    )


def solution(mesh):
    return jax.shard_map(
        on_device,
        mesh=mesh,
        in_specs=(
            P(("blk", "dp"), None),
            P(None, ("blk", "dp")),
            P(None, ("blk", "dp")),
            P(None, ("blk", "dp")),
            P(None, ("blk", "dp")),
            P(None, None, ("blk", "dp")),
            P(None, None, ("blk", "dp")),
            P(),
            P(),
            P(),
            P(),
            P(),
            P(),
            P(),
        ),
        out_specs=(P(("blk", "dp"), None), P(), P(), P(), P(), P(), P(), P()),
        check_vma=False,
    )
```

profile of v0, /device:TPU:0, one launch (start us, length us, event | category | flops | bytes accessed | tf_op | source)
XLA Modules:
  0.0 648.8 jit_solution(14372013255026179732)
XLA Ops:
  12.8 1.8 copy.68
  16.4 2.9 scatter_custom_fusion.1
  19.3 2.5 compare_select_fusion
  21.8 3.3 gather_fusion
  27.8 2.1 convolution_add_fusion.1
  29.9 2.4 convolution_add_fusion.3
  34.1 2.7 scatter_fusion
  38.6 3.2 collective-permute-start
  47.1 10.0 %gather_fusion.6 = f32[3840,172]{1,0:T(8,128)} fusion(f32[2048,172]{1,0:T(8,128)S(1)} %scatter_fusion, s32[4096]{0:T(1024)S(1)} %pad_clamp_fusion.1), kind=kCustom, calls=%fused_computation.6 | custom fusion | bytes 5299200 | tf_op jit(solution)/shard_map/jvp()/gather | solution.py:47
  57.2 3.5 copy.82
  60.7 12.4 %multiply_cosine_fusion = (f32[10,384,100]{1,2,0:T(8,128)}, f32[10,384,100]{1,2,0:T(8,128)S(1)}) fusion(f32[10,384]{1,0:T(8,128)S(1)} %fusion.64, f32[100]{0:T(128)} %param.22, f32[10,384]{1,0:T(8,128)S(1)} %fusion.66), kind=kLoop, calls=%fused_computation.40 | loop fusion | flops 768000 | bytes 3103120 | tf_op jit(solution)/shard_map/jvp()/cos | solution.py:49
  73.1 9.6 %fusion.5 = f32[10,384,344]{1,2,0:T(8,128)S(1)} fusion(f32[10,384,100]{1,2,0:T(8,128)S(1)} %get-tuple-element.135, f32[10,384,172]{1,2,0:T(8,128)S(1)} %copy.82, f32[272,344]{1,0:T(8,128)S(1)} %copy-done.18), kind=kOutput, calls=%fused_computation.29 | convolution fusion | flops 4312657920 | bytes 9836032 | tf_op jit(solution)/shard_map/jvp()/dot_general | solution.py:52
  82.8 2.3 copy-done.1
  86.9 2.5 reshape.869
  93.1 2.5 mul.438
  95.7 3.8 multiply_reduce_fusion.6
  102.5 1.8 broadcast_multiply_fusion.3
  106.0 3.0 reshape.871
  112.4 4.6 multiply_reduce_fusion.4
  119.9 10.7 %fusion.7 = f32[272,344]{1,0:T(8,128)} fusion(f32[10,384,172]{1,2,0:T(8,128)} %get-tuple-element.101, f32[10,384,172]{1,2,0:T(8,128)} %broadcast_multiply_fusion.3, f32[10,384,100]{1,2,0:T(8,128)} %copy-done.14, f32[10,384,172]{1,2,0:T(8,128)S(1)} %copy-done.6), kind=kOutput, calls=%fused_computation.51 | convolution fusion | flops 4313978880 | bytes 9836032 | tf_op jit(solution)/shard_map/transpose(jvp())/dot_general | solution.py:52
  130.6 11.5 %fusion.1 = f32[10,384,172]{2,1,0:T(8,128)} fusion(f32[10,384,172]{1,2,0:T(8,128)S(1)} %copy-done.10, f32[10,384,172]{1,2,0:T(8,128)S(1)} %copy-done.8, f32[272,344,1]{1,0,2:T(8,128)S(1)} %bitcast.110), kind=kOutput, calls=%fused_computation.23 | convolution fusion | flops 2727782400 | bytes 8318976 | tf_op jit(solution)/shard_map/transpose(jvp())/split | solution.py:50
  142.2 21.5 %scatter_custom_fusion.3 = f32[2048,172]{1,0:T(8,128)S(1)} fusion(s32[3840]{0:T(1024)} %copy-done.82, f32[3840,172]{1,0:T(8,128)} %bitcast.112, f32[]{:T(128)} %constant.19.clone.1), kind=kCustom, calls=%fused_computation.62 | custom fusion | flops 660480 | bytes 1409536 | tf_op jit(solution)/shard_map/transpose(jvp())/scatter-add | solution.py:47
  163.7 4.5 scatter_custom_fusion.4
  168.2 3.2 add_any.97
  171.5 2.8 gather_fusion.8
  174.9 2.2 fusion.21
  179.1 2.0 scatter_custom_fusion
  183.0 41.2 %all-reduce.23 = (f32[2,516]{1,0:T(2,128)S(1)}, f32[172]{0:T(256)S(1)}) all-reduce(f32[2,516]{1,0:T(2,128)S(1)} %pad_add_fusion.25, f32[172]{0:T(256)S(1)} %add_any.104), channel_id=1, replica_groups=mesh['blk'=8,'dp'=4] {'blk','dp'}, use_global_device_ids=true, to_apply=%region_19.21 | all-reduce | flops 1204 | bytes 9632 | tf_op jit(solution)/shard_map/psum | solution.py:80
  227.8 87.3 %all-reduce.31.cloned.1.call-done = (f32[444,516]{0,1:T(8,128)}, f32[172,516]{1,0:T(8,128)}, f32[272,344]{1,0:T(8,128)}, f32[172,172]{1,0:T(8,128)}) async-done(((f32[444,516]{0,1:T(8,128)}, f32[172,516]{1,0:T(8,128)}, f32[272,344]{1,0:T(8,128)}, f32[172,172]{1,0:T(8,128)}), (f32[444,516]{0,1:T(8,128)}, f32[172,516]{1,0:T(8,128)}, f32[272,344]{1,0:T(8,128)}, ...) | async-done | bytes 1764048 | tf_op jit(solution)/shard_map/psum | solution.py:80
  316.9 2.8 copy.76
  319.8 2.5 compare_select_fusion.1
  322.3 2.6 gather_fusion.5
  324.8 3.2 gather_fusion.4
  329.2 2.6 convolution_add_fusion
  335.7 2.7 scatter_fusion.1
  338.4 2.3 gather_fusion.9
  341.5 2.3 fusion.106
  345.5 10.5 %gather_fusion.10 = f32[3840,172]{1,0:T(8,128)} fusion(f32[2048,172]{1,0:T(8,128)S(1)} %scatter_fusion.1, s32[4096]{0:T(1024)} %pad_clamp_fusion), kind=kCustom, calls=%fused_computation.10 | custom fusion | bytes 5299200 | tf_op jit(solution)/shard_map/jvp()/gather | solution.py:47
  356.1 5.1 copy.94
  361.2 10.7 %fusion.4 = f32[10,384,344]{1,2,0:T(8,128)S(1)} fusion(f32[272,344,1]{1,0,2:T(8,128)} %fusion.58, f32[10,384,100]{1,2,0:T(8,128)} %get-tuple-element.134, f32[10,384,172]{1,2,0:T(8,128)} %copy.94), kind=kOutput, calls=%fused_computation.28 | convolution fusion | flops 4312657920 | bytes 9836032 | tf_op jit(solution)/shard_map/jvp()/dot_general | solution.py:52
  371.9 2.3 copy-done
  376.0 3.7 reshape.874
  379.7 2.0 multiply_reduce_fusion.3
  384.3 3.7 mul.489
  388.0 4.7 fusion.115
  395.8 1.8 broadcast_multiply_fusion.1
  399.2 3.7 reshape.876
  403.0 2.0 multiply_reduce_fusion.1
  406.9 3.9 broadcast_in_dim.101
  410.9 3.1 multiply_reduce_fusion
  416.0 7.8 %fusion.6 = f32[272,344]{1,0:T(8,128)} fusion(f32[10,384,172]{1,2,0:T(8,128)S(1)} %get-tuple-element.99, f32[10,384,172]{1,2,0:T(8,128)S(1)} %copy-done.9, f32[10,384,100]{1,2,0:T(8,128)S(1)} %copy-done.13, f32[10,384,172]{1,2,0:T(8,128)S(1)} %copy-done.7), kind=kOutput, calls=%fused_computation.50 | convolution fusion | flops 4313978880 | bytes 9836032 | tf_op jit(solution)/shard_map/transpose(jvp())/dot_general | solution.py:52
  423.8 11.8 %fusion.3 = f32[10,384,172]{2,1,0:T(8,128)} fusion(f32[10,384,172]{1,2,0:T(8,128)S(1)} %get-tuple-element.99, f32[10,384,172]{1,2,0:T(8,128)S(1)} %copy-done.9, f32[272,344,1]{1,0,2:T(8,128)S(1)} %copy-done.29), kind=kOutput, calls=%fused_computation.25 | convolution fusion | flops 2727782400 | bytes 8318976 | tf_op jit(solution)/shard_map/transpose(jvp())/split | solution.py:50
  436.5 22.2 %scatter_custom_fusion.6 = f32[2048,172]{1,0:T(8,128)} fusion(s32[3840]{0:T(1024)} %copy-done.81, f32[3840,172]{1,0:T(8,128)} %bitcast.111, f32[]{:T(128)} %constant.19.clone.1), kind=kCustom, calls=%fused_computation.58 | custom fusion | flops 660480 | bytes 1409536 | tf_op jit(solution)/shard_map/transpose(jvp())/scatter-add | solution.py:47
  458.8 4.7 scatter_custom_fusion.7
  463.5 3.8 add_any.112
  467.3 3.4 gather_fusion.11
  475.4 3.3 fusion.25
  486.0 67.1 %all-reduce.22 = (f32[1]{0:T(128)}, f32[1]{0:T(128)}, f32[2,516]{1,0:T(2,128)S(1)}, f32[172]{0:T(256)S(1)}) all-reduce(f32[1]{0:T(128)} %bitcast.27, f32[1]{0:T(128)} %bitcast.20, f32[2,516]{1,0:T(2,128)S(1)} %pad_add_fusion.24, f32[172]{0:T(256)S(1)} %add_any.119), channel_id=1, replica_groups=mesh['blk'=8,'dp'=4] {'blk','dp'}, use_global_device_ids=true, to_apply=%region_36.38 | all-reduce | flops 1206 | bytes 9648 | tf_op jit(solution)/shard_map/psum | solution.py:80
  553.7 1.9 pad_maximum_fusion.18
  556.1 75.7 %all-reduce.29.cloned.1.call-done = (f32[444,516]{0,1:T(8,128)}, f32[172,516]{1,0:T(8,128)}, f32[172,172]{1,0:T(8,128)}, f32[272,344]{1,0:T(8,128)}) async-done(((f32[444,516]{0,1:T(8,128)}, f32[172,516]{1,0:T(8,128)}, f32[172,172]{1,0:T(8,128)}, f32[272,344]{1,0:T(8,128)}), (f32[444,516]{0,1:T(8,128)}, f32[172,516]{1,0:T(8,128)}, f32[172,172]{1,0:T(8,128)}, ...) | async-done | bytes 1764048 | tf_op jit(solution)/shard_map/psum | solution.py:80
  631.8 1.8 multiply_subtract_fusion.7
  633.6 2.1 multiply_subtract_fusion.4
  635.7 1.8 multiply_subtract_fusion.2
  638.9 2.6 copy.131
  (366 shorter events, 79.0 us)
Async XLA Ops:
  7.2 308.0 %all-reduce.31.cloned.1.call-start = ((), (), s32[]{:S(2)}) async-start(), calls=%async_computation.1 | async-start | bytes 4227072 | tf_op jit(solution)/shard_map/psum | solution.py:80
  7.2 25.1 %copy-start.90 = (u32[256]{0:T(256)}, u32[256]{0:T(256)S(1)}, u32[]{:S(2)}) copy-start(u32[256]{0:T(256)S(1)} %iota_add_fusion) | copy-start | bytes 3076
  12.0 9.8 %copy-start.99 = (s32[1024]{0:T(1024)}, s32[1024]{0:T(1024)S(1)}, u32[]{:S(2)}) copy-start(s32[1024]{0:T(1024)S(1)} %pad_clamp_fusion.9) | copy-start | bytes 12292
  15.4 12.5 %copy-start.50 = (f32[128,172]{1,0:T(8,128)}, f32[128,172]{1,0:T(8,128)S(1)}, u32[]{:S(2)}) copy-start(f32[128,172]{1,0:T(8,128)S(1)} %gather_fusion.2) | copy-start | bytes 264196
  15.5 16.8 %copy-start.33 = (f32[128,172]{0,1:T(8,128)}, f32[128,172]{0,1:T(8,128)S(1)}, u32[]{:S(2)}) copy-start(f32[128,172]{0,1:T(8,128)S(1)} %copy.73) | copy-start | bytes 264196
  16.4 16.0 %copy-start.35 = (f32[128,172]{0,1:T(8,128)}, f32[128,172]{0,1:T(8,128)S(1)}, u32[]{:S(2)}) copy-start(f32[128,172]{0,1:T(8,128)S(1)} %copy.72) | copy-start | bytes 264196
  21.8 5.1 copy-start.111
  21.8 6.0 copy-start.11
  26.9 6.2 copy-start.70
  27.8 6.2 copy-start.75
  36.9 4.9 copy-start.112
  36.9 5.5 copy-start.87
  36.9 5.5 copy-start.88
  38.5 7.1 %copy-start.22 = (f32[172,172]{1,0:T(8,128)S(1)}, f32[172,172]{1,0:T(8,128)}, u32[]{:S(2)}) copy-start(f32[172,172]{1,0:T(8,128)} %param.26) | copy-start | bytes 355012
  38.6 278.4 %collective-permute-start = (f32[2048,172]{0,1:T(8,128)}, f32[2048,172]{0,1:T(8,128)}, u32[]{:S(2)}, u32[]{:S(2)}) collective-permute-start(f32[2048,172]{0,1:T(8,128)} %copy.75), channel_id=1, source_target_pairs={{0,4},{4,8},{8,12},{12,16},{16,20},{20,24},{24,28},{28,0},{1,5},{5... | collective-permute-start | bytes 4227080 | tf_op jit(solution)/shard_map/ppermute | solution.py:16
  46.3 10.9 %copy-start.30 = (f32[384,172]{0,1:T(8,128)}, f32[384,172]{0,1:T(8,128)S(1)}, u32[]{:S(2)}) copy-start(f32[384,172]{0,1:T(8,128)S(1)} %fusion.117) | copy-start | bytes 792580
  60.6 22.1 %copy-start.5 = (f32[10,384,172]{1,2,0:T(8,128)}, f32[10,384,172]{1,2,0:T(8,128)S(1)}, u32[]{:S(2)}) copy-start(f32[10,384,172]{1,2,0:T(8,128)S(1)} %copy.82) | copy-start | bytes 7925764
  60.7 12.5 %copy-start.18 = (f32[272,344]{1,0:T(8,128)S(1)}, f32[272,344]{1,0:T(8,128)}, u32[]{:S(2)}) copy-start(f32[272,344]{1,0:T(8,128)} %param.27) | copy-start | bytes 1122820
  73.1 9.6 %copy-start.14 = (f32[10,384,100]{1,2,0:T(8,128)}, f32[10,384,100]{1,2,0:T(8,128)S(1)}, u32[]{:S(2)}) copy-start(f32[10,384,100]{1,2,0:T(8,128)S(1)} %get-tuple-element.135) | copy-start | bytes 4608004
  112.4 6.1 copy-start.23
  112.4 6.1 copy-start.64
  112.4 6.1 copy-start.66
  112.4 6.1 copy-start.68
  112.4 7.5 %copy-start.6 = (f32[10,384,172]{1,2,0:T(8,128)S(1)}, f32[10,384,172]{1,2,0:T(8,128)}, u32[]{:S(2)}) copy-start(f32[10,384,172]{1,2,0:T(8,128)} %copy-done.5) | copy-start | bytes 7925764
  119.9 10.7 %copy-start.8 = (f32[10,384,172]{1,2,0:T(8,128)S(1)}, f32[10,384,172]{1,2,0:T(8,128)}, u32[]{:S(2)}) copy-start(f32[10,384,172]{1,2,0:T(8,128)} %broadcast_multiply_fusion.3) | copy-start | bytes 7925764
  119.9 10.7 %copy-start.10 = (f32[10,384,172]{1,2,0:T(8,128)S(1)}, f32[10,384,172]{1,2,0:T(8,128)}, u32[]{:S(2)}) copy-start(f32[10,384,172]{1,2,0:T(8,128)} %get-tuple-element.101) | copy-start | bytes 7925764
  178.6 45.5 %copy-start.109 = (s32[128]{0:T(128)S(1)}, s32[128]{0:T(128)}, u32[]{:S(2)}) copy-start(s32[128]{0:T(128)} %get-tuple-element.130) | copy-start | bytes 1540
  178.7 46.1 %copy-start.108 = (s32[128]{0:T(128)S(1)}, s32[128]{0:T(128)}, u32[]{:S(2)}) copy-start(s32[128]{0:T(128)} %get-tuple-element.128) | copy-start | bytes 1540
  178.7 46.7 %copy-start.113 = (s32[128]{0:T(128)S(1)}, s32[128]{0:T(128)}, u32[]{:S(2)}) copy-start(s32[128]{0:T(128)} %get-tuple-element.120) | copy-start | bytes 1540
  178.7 46.7 %copy-start.114 = (s32[128]{0:T(128)S(1)}, s32[128]{0:T(128)}, u32[]{:S(2)}) copy-start(s32[128]{0:T(128)} %get-tuple-element.142) | copy-start | bytes 1540
  178.7 453.1 %all-reduce.29.cloned.1.call-start = ((), (), s32[]{:S(2)}) async-start(), calls=%async_computation | async-start | bytes 4227072 | tf_op jit(solution)/shard_map/psum | solution.py:80
  179.0 48.2 %copy-start.89 = (f32[2,516]{1,0:T(2,128)S(1)}, f32[2,516]{1,0:T(2,128)}, u32[]{:S(2)}) copy-start(f32[2,516]{1,0:T(2,128)} %param.25) | copy-start | bytes 12388
  179.0 48.2 %copy-start.97 = (f32[172]{0:T(256)S(1)}, f32[172]{0:T(256)}, u32[]{:S(2)}) copy-start(f32[172]{0:T(256)} %param.28) | copy-start | bytes 2068
  179.1 137.8 %copy-start.98 = (s32[1024]{0:T(1024)}, s32[1024]{0:T(1024)S(1)}, u32[]{:S(2)}) copy-start(s32[1024]{0:T(1024)S(1)} %pad_clamp_fusion.6) | copy-start | bytes 12292
  181.2 135.8 %copy-start.3 = (u32[2048,172]{1,0:T(8,128)}, u32[2048,172]{1,0:T(8,128)S(1)}, u32[]{:S(2)}) copy-start(u32[2048,172]{1,0:T(8,128)S(1)} %scatter_custom_fusion) | copy-start | bytes 4227076
  181.2 138.6 %copy-start.81 = (s32[3840]{0:T(1024)}, s32[3840]{0:T(1024)S(1)}, u32[]{:S(2)}) copy-start(s32[3840]{0:T(1024)S(1)} %reshape.961) | copy-start | bytes 46084
  183.0 136.8 %copy-start.100 = (s32[384]{0:T(512)}, s32[384]{0:T(512)S(1)}, u32[]{:S(2)}) copy-start(s32[384]{0:T(512)S(1)} %fusion.70) | copy-start | bytes 4612
  227.2 92.6 %copy-start.85 = (f32[2,516]{1,0:T(2,128)}, f32[2,516]{1,0:T(2,128)S(1)}, u32[]{:S(2)}) copy-start(f32[2,516]{1,0:T(2,128)S(1)} %multiply_subtract_fusion.11) | copy-start | bytes 12388
  322.3 6.9 %copy-start.12 = (f32[444,516]{0,1:T(8,128)S(1)}, f32[444,516]{0,1:T(8,128)}, u32[]{:S(2)}) copy-start(f32[444,516]{0,1:T(8,128)} %param.23) | copy-start | bytes 2749252
  322.3 6.9 %copy-start.73 = (f32[128,100]{1,0:T(8,128)S(1)}, f32[128,100]{1,0:T(8,128)}, u32[]{:S(2)}) copy-start(f32[128,100]{1,0:T(8,128)} %get-tuple-element.136) | copy-start | bytes 153604
  324.8 8.1 %copy-start.49 = (f32[128,172]{1,0:T(8,128)}, f32[128,172]{1,0:T(8,128)S(1)}, u32[]{:S(2)}) copy-start(f32[128,172]{1,0:T(8,128)S(1)} %gather_fusion.5) | copy-start | bytes 264196
  329.0 5.6 copy-start.37
  329.1 5.5 copy-start.39
  388.0 4.7 copy-start.55
  388.0 4.8 copy-start.92
  388.0 7.7 %copy-start.2 = (f32[10,384,172]{1,2,0:T(8,128)S(1)}, f32[10,384,172]{1,2,0:T(8,128)}, u32[]{:S(2)}) copy-start(f32[10,384,172]{1,2,0:T(8,128)} %mul.489) | copy-start | bytes 7925764
  410.9 5.1 copy-start.7
  410.9 5.1 copy-start.9
  410.9 5.1 copy-start.13
  416.0 7.9 %copy-start.29 = (f32[272,344,1]{1,0,2:T(8,128)S(1)}, f32[272,344,1]{1,0,2:T(8,128)}, u32[]{:S(2)}) copy-start(f32[272,344,1]{1,0,2:T(8,128)} %fusion.58) | copy-start | bytes 1122820
  467.3 5.2 copy-start.38
  467.3 5.2 copy-start.40
  467.3 5.2 copy-start.72
  467.3 5.2 copy-start.117
  480.2 5.7 copy-start.106
  480.2 5.7 copy-start.107
  480.2 72.9 %copy-start.93 = (f32[172]{0:T(256)S(1)}, f32[172]{0:T(256)}, u32[]{:S(2)}) copy-start(f32[172]{0:T(256)} %multiply_subtract_fusion.13) | copy-start | bytes 2068
  480.2 75.3 %copy-start.86 = (f32[2,516]{1,0:T(2,128)S(1)}, f32[2,516]{1,0:T(2,128)}, u32[]{:S(2)}) copy-start(f32[2,516]{1,0:T(2,128)} %copy-done.85) | copy-start | bytes 12388
  480.3 151.6 %copy-start.25 = (f32[172,172]{1,0:T(8,128)S(1)}, f32[172,172]{1,0:T(8,128)}, u32[]{:S(2)}) copy-start(f32[172,172]{1,0:T(8,128)} %param.26) | copy-start | bytes 355012
  482.5 153.2 %copy-start.28 = (f32[172,516]{1,0:T(8,128)S(1)}, f32[172,516]{1,0:T(8,128)}, u32[]{:S(2)}) copy-start(f32[172,516]{1,0:T(8,128)} %param.24) | copy-start | bytes 1065028
  482.5 153.2 %copy-start.42 = (f32[172,516]{1,0:T(8,128)S(1)}, f32[172,516]{1,0:T(8,128)}, u32[]{:S(2)}) copy-start(f32[172,516]{1,0:T(8,128)} %get-tuple-element.73) | copy-start | bytes 1065028
  482.5 155.0 %copy-start.26 = (f32[444,516]{0,1:T(8,128)S(1)}, f32[444,516]{0,1:T(8,128)}, u32[]{:S(2)}) copy-start(f32[444,516]{0,1:T(8,128)} %get-tuple-element.72) | copy-start | bytes 2749252
  482.5 156.4 %collective-permute-start.1 = (f32[2048,172]{0,1:T(8,128)}, f32[2048,172]{0,1:T(8,128)}, u32[]{:S(2)}, u32[]{:S(2)}) collective-permute-start(f32[2048,172]{0,1:T(8,128)} %copy.91), channel_id=1, source_target_pairs={{0,4},{4,8},{8,12},{12,16},{16,20},{20,24},{24,28},{28,0},{1,5},{5... | collective-permute-start | bytes 4227080 | tf_op jit(solution)/shard_map/ppermute | solution.py:16
  631.8 5.7 copy-start.56
  (58 other events, 155.9 us)
Sparse Core Ops, SparseCore 0:
  178.7 136.3 all-reduce.30
  480.4 151.4 all-reduce.28
where the time goes:
time: 657 us; the launch traced here: 649 us
  waiting for transfers between devices  163 us (25%)
  other arithmetic  141 us (21%)
  local copies, waits for them, and re-layouts  129 us (20%)
  blocking collectives  108 us (16%)
  matrix products  85.7 us (13%)
  between operations  17.4 us (3%)
    psum x2, waiting for transfers between devices, summed_terms(): result = lax.psum(tuple(grads) + (loss,), ('blk', 'dp'))  163 us
    psum x2, blocking collectives, summed_terms(): result = lax.psum(tuple(grads) + (loss,), ('blk', 'dp'))  108 us
    scatter-add x2, other arithmetic, step_loss(): nbr_mem = updated[nbr_ids]  43.8 us
    dot_general x4, matrix products, step_loss(): jnp.dot(key_in.reshape(count_nbr * rows, -1), w_keyval, precision=exact,...  38.8 us
    gather x4, local copies, waits for them, and re-layouts, step_loss(): nbr_mem = updated[nbr_ids]  29.1 us
    split x2, matrix products, step_loss(): key_in = jnp.concatenate([nbr_mem, nenc], 2)  23.3 us
    gather x8, local copies, waits for them, and re-layouts, step_loss(): updated = memory.at[touched].set(fresh)  14.9 us
    unnamed x238, local copies, waits for them, and re-layouts  13.9 us
  transfers between devices with their start and end apart: 4, of which 2 were waited for; matrix products, arithmetic and copies ran while one was open for 24% of the time, Pallas kernels for 0%

commit v1 on v0

v1 whole, which is shorter than its diff:
```python
import jax
import jax.numpy as jnp
from jax import lax
from jax.experimental import pallas as pl
from jax.experimental.pallas import tpu as pltpu
from jax.sharding import PartitionSpec as P

HEADS = 2
STEPS = 2
AXES = ("blk", "dp")

rate = 0.25


def passed_along(shard, axis, by):
    devices = lax.axis_size(axis)
    return lax.ppermute(shard, axis, [(i, (i + by) % devices) for i in range(devices)])


def split2(x):
    hi = x.astype(jnp.bfloat16)
    lo = (x - hi.astype(jnp.float32)).astype(jnp.bfloat16)
    return hi, lo


def raw_dot(a, b, dims):
    return lax.dot_general(a, b, (dims, ((), ())), preferred_element_type=jnp.float32)


NN = ((1,), (0,))
NT = ((1,), (1,))
TN = ((0,), (0,))


def dot3(a, b, dims=NN):
    return raw_dot(a[0], b[0], dims) + (raw_dot(a[0], b[1], dims) + raw_dot(a[1], b[0], dims))


def dot_exact_left(a, b, dims=NN):
    return raw_dot(a, b[0], dims) + raw_dot(a, b[1], dims)


def dot_exact_right(a, b, dims=NN):
    return raw_dot(a[0], b, dims) + raw_dot(a[1], b, dims)


def up8(n):
    return -(-n // 8) * 8


class Packing:
    def __init__(self, width, tdim, devices):
        self.width, self.tdim = width, tdim
        self.a, self.b = up8(width), up8(tdim)
        self.b0 = 12 * self.a
        self.c0 = self.b0 + 5 * self.b
        unit = 8 * devices
        self.rows = -(-(self.c0 + 8) // unit) * unit

    def sec_a(self, i):
        return slice(i * self.a, i * self.a + self.width)

    def sec_b(self, i):
        return slice(self.b0 + i * self.b, self.b0 + i * self.b + self.tdim)

    def row(self, i):
        return slice(self.c0 + i, self.c0 + i + 1)

    def pack(self, w_input, w_hidden, gru_bias, w_query, w_keyval, w_decode):
        w = self.width
        gates = [slice(g * w, (g + 1) * w) for g in range(3)]
        a = [w_input[:w, s] for s in gates] + [w_input[w : 2 * w, s] for s in gates]
        a += [w_hidden[:, s] for s in gates] + [w_query, w_keyval[:w, :w], w_keyval[:w, w:]]
        b = [w_input[2 * w :, s] for s in gates] + [w_keyval[w:, :w], w_keyval[w:, w:]]
        pads = [jnp.pad(x, ((0, self.a - w), (0, 0))) for x in a]
        pads += [jnp.pad(x, ((0, self.b - self.tdim), (0, 0))) for x in b]
        tail = jnp.concatenate([gru_bias.reshape(6, w), w_decode[None, :]], 0)
        pads.append(jnp.pad(tail, ((0, self.rows - self.c0 - 7), (0, 0))))
        return jnp.concatenate(pads, 0)

    def unpack(self, p):
        a = [p[self.sec_a(i)] for i in range(12)]
        b = [p[self.sec_b(i)] for i in range(5)]
        w_input = jnp.concatenate(
            [jnp.concatenate([a[g], a[3 + g], b[g]], 0) for g in range(3)], 1
        )
        w_hidden = jnp.concatenate(a[6:9], 1)
        w_keyval = jnp.concatenate(
            [jnp.concatenate([a[10], b[3]], 0), jnp.concatenate([a[11], b[4]], 0)], 1
        )
        bias = p[self.c0 : self.c0 + 6].reshape(2, 3 * self.width)
        return w_input, w_hidden, bias, a[9], w_keyval, p[self.c0 + 6]


def gru_kernel(pk, h_ref, h2_ref, e2_ref, p_ref, fresh_ref, save_ref):
    h = h_ref[...]
    hs, h2s, es = split2(h), split2(h2_ref[...]), split2(e2_ref[...])

    def gates(g):
        gi = dot3(hs, split2(p_ref[pk.sec_a(g), :]))
        gi += dot3(h2s, split2(p_ref[pk.sec_a(3 + g), :]))
        gi += dot3(es, split2(p_ref[pk.sec_b(g), :]))
        gi += p_ref[pk.row(g), :]
        gh = dot3(hs, split2(p_ref[pk.sec_a(6 + g), :])) + p_ref[pk.row(3 + g), :]
        return gi, gh

    gi, gh = gates(0)
    reset = jax.nn.sigmoid(gi + gh)
    gi, gh = gates(1)
    update = jax.nn.sigmoid(gi + gh)
    gi, gh = gates(2)
    cand = jnp.tanh(gi + reset * gh)
    fresh_ref[...] = (1.0 - update) * cand + update * h
    save_ref[0] = reset
    save_ref[1] = update
    save_ref[2] = cand
    save_ref[3] = gh


def softplus(x):
    return jnp.maximum(x, 0.0) + jnp.log1p(jnp.exp(-jnp.abs(x)))


def attn_kernel(
    pk, inv_count, h_ref, h2_ref, e2_ref, fresh_ref, save_ref, negm_ref, nbrm_ref, nenc_ref,
    touched_ref, negid_ref, nbrid_ref, p_ref, g_ref, nm_ref, k_ref, v_ref, s_ref,
):
    n_nbr, rows, width = nbrm_ref.shape
    both = h_ref.shape[0]
    events = both // 2
    head = width // HEADS
    inv_root = 1.0 / (head**0.5)
    bf = jnp.bfloat16
    touched = touched_ref[...]

    def onehot(ids):
        hit = (ids == touched).astype(jnp.float32)
        return hit.astype(bf), 1.0 - jnp.max(hit, axis=1, keepdims=True)

    ri = lax.broadcasted_iota(jnp.int32, (width, width), 0) // head
    ci = lax.broadcasted_iota(jnp.int32, (width, width), 1) // head
    same = (ri == ci).astype(jnp.float32).astype(bf)

    def head_sum(x):
        return dot_exact_right(split2(x), same)

    g_ref[...] = jnp.zeros(g_ref.shape, jnp.float32)
    fresh = fresh_ref[...]
    fs = split2(fresh)
    o_neg, keep = onehot(negid_ref[...])
    neg_mem = negm_ref[...] * keep + dot_exact_left(o_neg, fs)
    qmem = jnp.concatenate([fresh, neg_mem], 0)
    qms = split2(qmem)
    wq = split2(p_ref[pk.sec_a(9), :])
    query = dot3(qms, wq) * inv_root
    wk1 = split2(p_ref[pk.sec_a(10), :])
    wv1 = split2(p_ref[pk.sec_a(11), :])
    wk2 = split2(p_ref[pk.sec_b(3), :])
    wv2 = split2(p_ref[pk.sec_b(4), :])

    top = None
    for j in range(n_nbr):
        o_j, keep = onehot(nbrid_ref[j])
        mem = nbrm_ref[j] * keep + dot_exact_left(o_j, fs)
        nm_ref[j] = mem
        ms = split2(mem)
        ns = split2(nenc_ref[j])
        key = dot3(ms, wk1) + dot3(ns, wk2)
        k_ref[j] = key
        v_ref[j] = dot3(ms, wv1) + dot3(ns, wv2)
        score = head_sum(key * query)
        s_ref[j] = score
        top = score if top is None else jnp.maximum(top, score)
    den = jnp.zeros_like(top)
    acc = jnp.zeros_like(top)
    for j in range(n_nbr):
        prob = jnp.exp(s_ref[j] - top)
        s_ref[j] = prob
        den += prob
        acc += prob * v_ref[j]
    inv_den = 1.0 / den
    attn = acc * inv_den
    embed = qmem + attn
    e_s, e_d, e_n = embed[:events], embed[events:both], embed[both:]
    w_dec = p_ref[pk.row(6), :]
    sw = e_s * w_dec
    pos = jnp.sum(sw * e_d, axis=1, keepdims=True)
    neg = jnp.sum(sw * e_n, axis=1, keepdims=True)
    loss = jnp.sum(softplus(-pos) + softplus(neg), axis=0, keepdims=True) * inv_count
    d_pos = -jax.nn.sigmoid(-pos) * inv_count
    d_neg = jax.nn.sigmoid(neg) * inv_count
    mix = d_pos * e_d + d_neg * e_n
    g_ref[pk.row(6), :] = jnp.sum(e_s * mix, axis=0, keepdims=True)
    g_ref[pk.row(7), :] = jnp.broadcast_to(loss, (1, width))
    d_embed = jnp.concatenate([mix * w_dec, d_pos * sw, d_neg * sw], 0)

    mean_dp = head_sum(d_embed * attn)
    d_query = jnp.zeros_like(query)
    r_k = jnp.zeros((both, width), jnp.float32)
    r_v = jnp.zeros((both, width), jnp.float32)
    for j in range(n_nbr):
        prob = s_ref[j] * inv_den
        d_score = prob * (head_sum(d_embed * v_ref[j]) - mean_dp)
        d_query += d_score * k_ref[j]
        d_key = split2(d_score * query)
        d_val = split2(prob * d_embed)
        ms = split2(nm_ref[j])
        ns = split2(nenc_ref[j])
        g_ref[pk.sec_a(10), :] += dot3(ms, d_key, TN)
        g_ref[pk.sec_a(11), :] += dot3(ms, d_val, TN)
        g_ref[pk.sec_b(3), :] += dot3(ns, d_key, TN)
        g_ref[pk.sec_b(4), :] += dot3(ns, d_val, TN)
        o_j = (nbrid_ref[j] == touched).astype(jnp.float32).astype(bf)
        r_k += dot_exact_left(o_j, d_key, TN)
        r_v += dot_exact_left(o_j, d_val, TN)
    dqs = split2(d_query * inv_root)
    g_ref[pk.sec_a(9), :] = dot3(qms, dqs, TN)
    d_qmem = d_embed + dot3(dqs, wq, NT)
    d_fresh = d_qmem[:both] + dot_exact_left(o_neg, split2(d_qmem[both:]), TN)
    d_fresh += dot3(split2(r_k), wk1, NT) + dot3(split2(r_v), wv1, NT)

    h = h_ref[...]
    reset, update, cand, gh_n = save_ref[0], save_ref[1], save_ref[2], save_ref[3]
    d_z = d_fresh * (h - cand) * update * (1.0 - update)
    d_n = d_fresh * (1.0 - update) * (1.0 - cand * cand)
    d_hn = d_n * reset
    d_r = d_n * gh_n * reset * (1.0 - reset)
    hs, h2s, es = split2(h), split2(h2_ref[...]), split2(e2_ref[...])
    for g, d in enumerate((d_r, d_z, d_n)):
        ds = split2(d)
        by_h = dot3(hs, ds, TN)
        g_ref[pk.sec_a(g), :] = by_h
        g_ref[pk.sec_a(3 + g), :] = dot3(h2s, ds, TN)
        g_ref[pk.sec_b(g), :] = dot3(es, ds, TN)
        d_bias = jnp.sum(d, axis=0, keepdims=True)
        g_ref[pk.row(g), :] = d_bias
        if g < 2:
            g_ref[pk.sec_a(6 + g), :] = by_h
            g_ref[pk.row(3 + g), :] = d_bias
        else:
            g_ref[pk.sec_a(8), :] = dot3(hs, split2(d_hn), TN)
            g_ref[pk.row(5), :] = jnp.sum(d_hn, axis=0, keepdims=True)


VMEM_LIMIT = 56 * 1024 * 1024


def gru(pk, h, h2, e2, p):
    shape = jax.ShapeDtypeStruct(h.shape, jnp.float32)
    saved = jax.ShapeDtypeStruct((4,) + h.shape, jnp.float32)
    return pl.pallas_call(
        lambda *refs: gru_kernel(pk, *refs),
        out_shape=(shape, saved),
        compiler_params=pltpu.CompilerParams(vmem_limit_bytes=VMEM_LIMIT),
        name="gru",
    )(h, h2, e2, p)


def attention(pk, inv_count, *args):
    big = pltpu.VMEM(args[6].shape, jnp.float32)
    return pl.pallas_call(
        lambda *refs: attn_kernel(pk, inv_count, *refs),
        out_shape=jax.ShapeDtypeStruct(args[-1].shape, jnp.float32),
        scratch_shapes=[big] * 4,
        compiler_params=pltpu.CompilerParams(vmem_limit_bytes=VMEM_LIMIT),
        name="attention",
    )(*args)


def summed(grads):
    return lax.psum(grads, AXES)


def on_device(
    memory,
    src,
    dst,
    negative,
    event_time,
    neighbours,
    neighbour_time,
    time_omega,
    *weights,
):
    width, tdim = memory.shape[1], time_omega.shape[0]
    n_dev = lax.axis_size("blk") * lax.axis_size("dp")
    pk = Packing(width, tdim, n_dev)
    inv_count = 1.0 / float(src.shape[1] * n_dev)
    params = pk.pack(*weights)
    losses = []
    for step in range(STEPS):
        events = src.shape[1]
        n_nbr, rows = neighbours.shape[1:]
        touched = jnp.concatenate([src[step], dst[step]], 0)
        h = memory.at[touched].get(mode="promise_in_bounds")
        h2 = jnp.concatenate([h[events:], h[:events]], 0)
        negm = memory.at[negative[step]].get(mode="promise_in_bounds")
        nbrm = memory.at[neighbours[step].reshape(-1)].get(mode="promise_in_bounds")
        nbrm = nbrm.reshape(n_nbr, rows, width)
        stamp = event_time[step].astype(jnp.float32)
        tenc = jnp.cos(stamp[:, None] * time_omega[None, :])
        e2 = jnp.concatenate([tenc, tenc], 0)
        row_time = jnp.concatenate([stamp, stamp, stamp], 0)
        delta = row_time[None, :] - neighbour_time[step].astype(jnp.float32)
        nenc = jnp.cos(delta[:, :, None] * time_omega[None, None, :])
        fresh, saved = gru(pk, h, h2, e2, params)
        updated = memory.at[touched].set(
            fresh, mode="promise_in_bounds", unique_indices=True
        )
        memory = passed_along(updated, "blk", 1)
        grads = attention(
            pk, inv_count, h, h2, e2, fresh, saved, negm, nbrm, nenc,
            touched[None, :], negative[step][:, None], neighbours[step][:, :, None], params,
        )
        sums = summed(grads)
        losses.append(sums[pk.c0 + 7, 0])
        params = params - rate * sums
    return (memory, jnp.stack(losses)) + pk.unpack(params)


def solution(mesh):
    rows = P(("blk", "dp"), None)
    ids = P(None, ("blk", "dp"))
    nbrs = P(None, None, ("blk", "dp"))
    return jax.shard_map(
        on_device,
        mesh=mesh,
        in_specs=(rows, ids, ids, ids, ids, nbrs, nbrs) + (P(),) * 7,
        out_specs=(rows,) + (P(),) * 7,
        check_vma=False,
    )
```

time: 657 us -> 489 us (0.74)
  waiting for transfers between devices: 163 us -> 273 us
  blocking collectives: 108 us -> 0 us
  other arithmetic: 141 us -> 40.3 us
  matrix products: 85.7 us -> 0 us
  Pallas kernels: 0 us -> 69.3 us
  local copies, waits for them, and re-layouts: 129 us -> 81.7 us
    psum x2, waiting for transfers between devices: 163 us -> 273 us  [summed(): return lax.psum(grads, AXES)]
    psum x2 -> x0, blocking collectives: 108 us -> none  [summed_terms(): result = lax.psum(tuple(grads) + (loss,), ('blk', 'dp'))]
    pallas_call x0 -> x4, Pallas kernels: none -> 69.3 us  [the longest x2 60.4 us: attention(): pl.pallas_call(lambda *refs: attn_kernel(pk, inv_count, *refs), out_shape...]
    dot_general x18 -> x0, matrix products: 62.4 us -> none  [the longest x4 38.8 us: step_loss(): jnp.dot(key_in.reshape(count_nbr * rows, -1), w_keyval, precision=exact,...]
    scatter-add x6 -> x0, other arithmetic: 58.4 us -> none  [the longest x2 43.8 us: step_loss(): nbr_mem = updated[nbr_ids]]
    gather x24 -> x6, local copies, waits for them, and re-layouts: 58.2 us -> 25.3 us  [the longest x2 20.3 us: on_device(): nbrm = memory.at[neighbours[step].reshape(-1)].get(mode='promise_in_bounds')]
    split x2 -> x0, matrix products: 23.3 us -> none  [step_loss(): key_in = jnp.concatenate([nbr_mem, nenc], 2)]
    reduce_sum x18 -> x0, other arithmetic: 20.7 us -> none  [the longest x4 10.9 us: step_loss(): scores = jnp.sum(keys * query[None], -1) / jnp.sqrt(jnp.float32(head_size))]
  transfers between devices with their start and end apart: 4 -> 4, of which waited for: 2 -> 2; matrix products, arithmetic and copies ran while one was open for 24% -> 7% of each run, Pallas kernels for 0% -> 0%
where the time goes in v1:
time: 489 us; the launch traced here: 484 us
  waiting for transfers between devices  273 us (56%)
  local copies, waits for them, and re-layouts  81.7 us (17%)
  Pallas kernels  69.3 us (14%)
  other arithmetic  40.3 us (8%)
  between operations  14.8 us (3%)
    psum x2, waiting for transfers between devices, summed(): return lax.psum(grads, AXES)  273 us
    pallas_call x2, Pallas kernels, attention(): pl.pallas_call(lambda *refs: attn_kernel(pk, inv_count, *refs), out_shape...  60.4 us
    unnamed x125, local copies, waits for them, and re-layouts  27 us
    gather x2, local copies, waits for them, and re-layouts, on_device(): nbrm = memory.at[neighbours[step].reshape(-1)].get(mode='promise_in_bounds')  20.3 us
    cos x1, other arithmetic, on_device(): nenc = jnp.cos(delta[:, :, None] * time_omega[None, None, :])  14.6 us
  transfers between devices with their start and end apart: 4, of which 2 were waited for; matrix products, arithmetic and copies ran while one was open for 7% of the time, Pallas kernels for 0%

profile of v1, /device:TPU:0, one launch (start us, length us, event | category | flops | bytes accessed | tf_op | source)
XLA Modules:
  0.0 483.8 jit_solution(16224253710725747036)
XLA Ops:
  7.2 1.6 fusion.12
  8.9 2.0 fusion.11
  10.9 0.8 fusion.15
  11.7 0.7 fusion.14
  14.4 0.8 copy.113
  15.2 0.8 copy.114
  16.0 0.8 copy.115
  16.8 0.8 copy.116
  17.6 0.8 copy.117
  18.3 0.9 fusion.13
  19.2 0.7 copy.118
  20.0 0.8 copy.119
  20.7 0.8 copy.120
  22.2 0.8 copy.96
  23.1 1.0 gather_fusion
  24.1 0.8 fusion.17
  25.5 0.9 multiply_cosine_fusion.2
  28.4 10.1 %gather_fusion.3 = f32[3840,172]{1,0:T(8,128)} fusion(f32[2048,172]{1,0:T(8,128)S(1)} %copy.96, s32[4096]{0:T(1024)S(1)} %pad_clamp_fusion.1), kind=kCustom, calls=%fused_computation.3 | custom fusion | bytes 5299200 | tf_op jit(solution)/shard_map/gather | solution.py:298
  38.6 1.4 gather_fusion.2
  40.0 2.7 copy.103.refs_10_
  42.8 0.7 copy.102.refs_9_
  45.0 0.7 pad_dynamic-update-slice_fusion.8
  46.4 0.7 pad_dynamic-update-slice_fusion.6
  47.1 1.6 pad_dynamic-update-slice_fusion.5
  48.7 1.6 pad_dynamic-update-slice_fusion.4
  50.3 1.6 pad_dynamic-update-slice_fusion.3
  53.3 0.7 pad_dynamic-update-slice_fusion
  57.3 1.7 pad_maximum_fusion.1.refs_1_
  59.6 14.6 %multiply_cosine_fusion = (f32[10,384,100]{2,1,0:T(8,128)}, f32[10,384,100]{2,1,0:T(8,128)}) fusion(f32[10,384]{1,0:T(8,128)S(1)} %fusion.2, f32[100]{0:T(128)S(1)} %copy-done.39, f32[10,384]{1,0:T(8,128)S(1)} %fusion.4), kind=kLoop, calls=%fused_computation.10 | loop fusion | flops 768000 | bytes 3103120 | tf_op jit(solution)/shard_map/cos | solution.py:305
  74.9 4.5 gru.2
  79.4 30.3 %attention.2 = f32[2816,172]{1,0:T(8,128)} custom-call(f32[256,172]{1,0:T(8,128)} %copy-done, f32[256,172]{1,0:T(8,128)} %pad_maximum_fusion.1.refs_1_, f32[256,100]{1,0:T(8,128)} %pad_maximum_fusion.3.refs_2_, f32[256,172]{1,0:T(8,128)} %get-tuple-element.12.refs_3_, f32[4,256,172]{2,1,0:T(8,128)} %get-tuple-element.13.refs_4_, f32[128,172]{1,0:T(8,128)} %gather_fusion.2, ...), custom_call_target="tpu_custom_call" | custom-call | tf_op jit(solution)/shard_map/attention/pallas_call | solution.py:261
  109.8 0.9 copy-done.4
  110.6 2.2 scatter_fusion
  112.8 0.8 copy.97
  113.6 3.0 collective-permute-start
  118.5 1.3 pad_add_fusion.1
  119.8 1.9 copy.110.refs_10_
  121.6 1.3 copy.109.refs_9_
  123.0 1.3 pad_clamp_fusion.2
  124.3 0.8 fusion.6
  125.0 1.6 pad_maximum_fusion.4.refs_2_
  126.6 132.9 %all-reduce.21.cloned.1.call-done = f32[2816,172]{1,0:T(8,128)} async-done(((f32[2816,172]{1,0:T(8,128)}), f32[2816,172]{1,0:T(8,128)}) %all-reduce.21.cloned.1.call-update) | async-done | bytes 1937424 | tf_op jit(solution)/shard_map/psum | solution.py:271
  259.6 4.7 multiply_subtract_fusion.1.refs_3_.refs_11_
  264.3 1.8 copy.104
  266.1 1.1 gather_fusion.1
  267.3 10.2 %gather_fusion.5 = f32[3840,172]{1,0:T(8,128)} fusion(f32[2048,172]{1,0:T(8,128)S(1)} %copy.104, s32[4096]{0:T(1024)S(1)} %pad_clamp_fusion), kind=kCustom, calls=%fused_computation.5 | custom fusion | bytes 5299200 | tf_op jit(solution)/shard_map/gather | solution.py:298
  277.5 1.5 gather_fusion.4
  279.0 0.7 pad_maximum_fusion.2.refs_1_
  279.8 4.5 gru.3
  284.2 30.0 %attention.3 = f32[2816,172]{1,0:T(8,128)} custom-call(f32[256,172]{1,0:T(8,128)} %copy-done.1, f32[256,172]{1,0:T(8,128)} %pad_maximum_fusion.2.refs_1_, f32[256,100]{1,0:T(8,128)} %pad_maximum_fusion.4.refs_2_, f32[256,172]{1,0:T(8,128)} %get-tuple-element.14.refs_3_, f32[4,256,172]{2,1,0:T(8,128)} %get-tuple-element.15.refs_4_, f32[128,172]{1,0:T(8,128)} %gather_fusion.4, ...), custom_call_target="tpu_custom_call" | custom-call | tf_op jit(solution)/shard_map/attention/pallas_call | solution.py:261
  314.3 1.3 slice.232
  315.6 2.2 scatter_fusion.1
  317.8 0.8 copy.105
  318.6 1.6 collective-permute-start.1
  320.2 140.0 %all-reduce.23.cloned.1.call-done = f32[2816,172]{1,0:T(8,128)} async-done(((f32[2816,172]{1,0:T(8,128)}), f32[2816,172]{1,0:T(8,128)}) %all-reduce.23.cloned.1.call-update) | async-done | bytes 1937424 | tf_op jit(solution)/shard_map/psum | solution.py:271
  460.2 3.1 multiply_subtract_fusion
  463.9 0.7 fusion.10
  464.6 1.0 fusion.9
  466.1 1.3 copy.111
  468.1 1.2 slice.233
  469.3 1.9 pad_maximum_fusion.7
  471.1 2.0 maximum_maximum_fusion.1
  473.2 1.0 pad_maximum_fusion
  474.1 2.6 copy.155
  (139 shorter events, 17.0 us)
Async XLA Ops:
  7.2 3.7 copy-start.5
  7.2 5.3 %copy-start.37 = (s32[2,128]{1,0:T(2,128)S(1)}, s32[2,128]{1,0:T(2,128)}, u32[]{:S(2)}) copy-start(s32[2,128]{1,0:T(2,128)} %param.17) | copy-start | bytes 3076
  7.2 11.2 %copy-start.16 = (f32[172,516]{1,0:T(8,128)S(1)}, f32[172,516]{1,0:T(8,128)}, u32[]{:S(2)}) copy-start(f32[172,516]{1,0:T(8,128)} %param.23) | copy-start | bytes 1065028
  7.2 252.4 %all-reduce.21.cloned.1.call-start = ((), (), s32[]{:S(2)}) async-start(), calls=%async_computation | async-start | bytes 5767168 | tf_op jit(solution)/shard_map/psum | solution.py:271
  8.8 12.7 %copy-start.36 = (f32[2,516]{1,0:T(2,128)S(1)}, f32[2,516]{1,0:T(2,128)}, u32[]{:S(2)}) copy-start(f32[2,516]{1,0:T(2,128)} %param.24) | copy-start | bytes 12388
  8.9 12.7 %copy-start.46 = (s32[2,128]{1,0:T(2,128)S(1)}, s32[2,128]{1,0:T(2,128)}, u32[]{:S(2)}) copy-start(s32[2,128]{1,0:T(2,128)} %param.16) | copy-start | bytes 3076
  8.9 12.7 %copy-start.47 = (s32[2,128]{1,0:T(2,128)S(1)}, s32[2,128]{1,0:T(2,128)}, u32[]{:S(2)}) copy-start(s32[2,128]{1,0:T(2,128)} %param.15) | copy-start | bytes 3076
  8.9 13.3 %copy-start.2 = (f32[2048,172]{0,1:T(8,128)S(1)}, f32[2048,172]{0,1:T(8,128)}, u32[]{:S(2)}) copy-start(f32[2048,172]{0,1:T(8,128)} %param.14) | copy-start | bytes 4227076
  12.4 6.8 %copy-start.23 = (f32[100,172]{0,1:T(8,128)S(1)}, f32[100,172]{0,1:T(8,128)}, u32[]{:S(2)}) copy-start(f32[100,172]{0,1:T(8,128)} %get-tuple-element.67) | copy-start | bytes 206404
  12.4 7.6 %copy-start.22 = (f32[100,172]{0,1:T(8,128)S(1)}, f32[100,172]{0,1:T(8,128)}, u32[]{:S(2)}) copy-start(f32[100,172]{0,1:T(8,128)} %get-tuple-element.66) | copy-start | bytes 206404
  22.2 1.9 copy-start.30
  23.0 1.9 copy-start.45
  23.0 2.5 copy-start.38
  23.0 4.0 copy-start.28
  23.1 4.6 copy-start.29
  24.1 14.5 %copy-start = (f32[256,172]{1,0:T(8,128)}, f32[256,172]{1,0:T(8,128)S(1)}, u32[]{:S(2)}) copy-start(f32[256,172]{1,0:T(8,128)S(1)} %gather_fusion) | copy-start | bytes 528388
  28.4 10.2 %copy-start.43 = (s32[128]{0:T(128)S(1)}, s32[128]{0:T(128)}, u32[]{:S(2)}) copy-start(s32[128]{0:T(128)} %get-tuple-element.102) | copy-start | bytes 1540
  38.5 5.0 %copy-start.12 = (f32[172,172]{1,0:T(8,128)S(1)}, f32[172,172]{1,0:T(8,128)}, u32[]{:S(2)}) copy-start(f32[172,172]{1,0:T(8,128)} %copy.113) | copy-start | bytes 355012
  38.5 5.7 %copy-start.13 = (f32[172,172]{1,0:T(8,128)S(1)}, f32[172,172]{1,0:T(8,128)}, u32[]{:S(2)}) copy-start(f32[172,172]{1,0:T(8,128)} %copy.114) | copy-start | bytes 355012
  38.5 6.4 %copy-start.11 = (f32[172,172]{1,0:T(8,128)S(1)}, f32[172,172]{1,0:T(8,128)}, u32[]{:S(2)}) copy-start(f32[172,172]{1,0:T(8,128)} %copy.115) | copy-start | bytes 355012
  38.6 7.1 %copy-start.9 = (f32[172,172]{1,0:T(8,128)S(1)}, f32[172,172]{1,0:T(8,128)}, u32[]{:S(2)}) copy-start(f32[172,172]{1,0:T(8,128)} %copy.116) | copy-start | bytes 355012
  38.6 7.8 %copy-start.10 = (f32[172,172]{1,0:T(8,128)S(1)}, f32[172,172]{1,0:T(8,128)}, u32[]{:S(2)}) copy-start(f32[172,172]{1,0:T(8,128)} %copy.117) | copy-start | bytes 355012
  38.6 4.2 copy-start.40
  40.0 12.6 %copy-start.15 = (f32[172,172]{1,0:T(8,128)S(1)}, f32[172,172]{1,0:T(8,128)}, u32[]{:S(2)}) copy-start(f32[172,172]{1,0:T(8,128)} %get-tuple-element.80) | copy-start | bytes 355012
  40.0 13.3 %copy-start.14 = (f32[172,172]{1,0:T(8,128)S(1)}, f32[172,172]{1,0:T(8,128)}, u32[]{:S(2)}) copy-start(f32[172,172]{1,0:T(8,128)} %get-tuple-element.79) | copy-start | bytes 355012
  40.0 14.6 %copy-start.17 = (f32[100,172]{1,0:T(8,128)S(1)}, f32[100,172]{1,0:T(8,128)}, u32[]{:S(2)}) copy-start(f32[100,172]{1,0:T(8,128)} %copy.119) | copy-start | bytes 206404
  42.8 16.2 %copy-start.41 = (s32[128]{0:T(128)S(1)}, s32[128]{0:T(128)}, u32[]{:S(2)}) copy-start(s32[128]{0:T(128)} %get-tuple-element.98) | copy-start | bytes 1540
  42.8 16.2 %copy-start.42 = (s32[128]{0:T(128)S(1)}, s32[128]{0:T(128)}, u32[]{:S(2)}) copy-start(s32[128]{0:T(128)} %get-tuple-element.111) | copy-start | bytes 1540
  42.8 16.8 %copy-start.27 = (s32[1,10,384]{2,0,1:T(1,128)S(1)}, s32[1,10,384]{2,0,1:T(1,128)}, u32[]{:S(2)}) copy-start(s32[1,10,384]{2,0,1:T(1,128)} %get-tuple-element.89) | copy-start | bytes 46084
  42.8 16.8 %copy-start.35 = (f32[384]{0:T(512)S(1)}, f32[384]{0:T(512)}, u32[]{:S(2)}) copy-start(f32[384]{0:T(512)} %get-tuple-element.114) | copy-start | bytes 4612
  42.8 16.8 %copy-start.26 = (s32[1,10,384]{2,0,1:T(1,128)S(1)}, s32[1,10,384]{2,0,1:T(1,128)}, u32[]{:S(2)}) copy-start(s32[1,10,384]{2,0,1:T(1,128)} %get-tuple-element.90) | copy-start | bytes 46084
  42.8 16.8 %copy-start.34 = (f32[384]{0:T(512)S(1)}, f32[384]{0:T(512)}, u32[]{:S(2)}) copy-start(f32[384]{0:T(512)} %get-tuple-element.113) | copy-start | bytes 4612
  42.8 16.8 %copy-start.39 = (f32[100]{0:T(128)S(1)}, f32[100]{0:T(128)}, u32[]{:S(2)}) copy-start(f32[100]{0:T(128)} %param.21) | copy-start | bytes 1204
  43.6 8.3 %copy-start.24 = (f32[172,172]{1,0:T(8,128)S(1)}, f32[172,172]{1,0:T(8,128)}, u32[]{:S(2)}) copy-start(f32[172,172]{1,0:T(8,128)} %param.25) | copy-start | bytes 355012
  43.6 10.4 %copy-start.19 = (f32[100,172]{1,0:T(8,128)S(1)}, f32[100,172]{1,0:T(8,128)}, u32[]{:S(2)}) copy-start(f32[100,172]{1,0:T(8,128)} %copy.118) | copy-start | bytes 206404
  43.6 11.7 %copy-start.18 = (f32[100,172]{1,0:T(8,128)S(1)}, f32[100,172]{1,0:T(8,128)}, u32[]{:S(2)}) copy-start(f32[100,172]{1,0:T(8,128)} %copy.120) | copy-start | bytes 206404
  43.6 12.4 %copy-start.21 = (f32[100,172]{1,0:T(8,128)S(1)}, f32[100,172]{1,0:T(8,128)}, u32[]{:S(2)}) copy-start(f32[100,172]{1,0:T(8,128)} %get-tuple-element.78) | copy-start | bytes 206404
  43.6 13.0 %copy-start.20 = (f32[100,172]{1,0:T(8,128)S(1)}, f32[100,172]{1,0:T(8,128)}, u32[]{:S(2)}) copy-start(f32[100,172]{1,0:T(8,128)} %get-tuple-element.77) | copy-start | bytes 206404
  54.0 20.2 %copy-start.44 = (f32[172]{0:T(256)S(1)}, f32[172]{0:T(256)}, u32[]{:S(2)}) copy-start(f32[172]{0:T(256)} %param.27) | copy-start | bytes 2068
  109.7 0.9 copy-start.4
  109.7 1.0 copy-start.31
  109.7 350.5 %all-reduce.23.cloned.1.call-start = ((), (), s32[]{:S(2)}) async-start(), calls=%async_computation.1 | async-start | bytes 5767168 | tf_op jit(solution)/shard_map/psum | solution.py:271
  112.8 7.0 %copy-start.25 = (s32[10,384,1]{1,2,0:T(1,128)S(1)}, s32[10,384,1]{1,2,0:T(1,128)}, u32[]{:S(2)}) copy-start(s32[10,384,1]{1,2,0:T(1,128)} %get-tuple-element.85) | copy-start | bytes 46084
  113.6 150.7 %collective-permute-start = (f32[2048,172]{0,1:T(8,128)S(1)}, f32[2048,172]{0,1:T(8,128)}, u32[]{:S(2)}, u32[]{:S(2)}) collective-permute-start(f32[2048,172]{0,1:T(8,128)S(1)} %copy.97), channel_id=1, source_target_pairs={{0,4},{4,8},{8,12},{12,16},{16,20},{20,24},{24,28},{28,0},{1,5},{5... | collective-permute-start | bytes 4227080 | tf_op jit(solution)/shard_map/ppermute | solution.py:17
  117.3 0.6 copy-start.32
  267.2 10.3 %copy-start.1 = (f32[256,172]{1,0:T(8,128)}, f32[256,172]{1,0:T(8,128)S(1)}, u32[]{:S(2)}) copy-start(f32[256,172]{1,0:T(8,128)S(1)} %gather_fusion.1) | copy-start | bytes 528388
  314.3 1.3 copy-start.3
  314.3 1.3 copy-start.33
  318.6 155.5 %collective-permute-start.1 = (f32[2048,172]{0,1:T(8,128)S(1)}, f32[2048,172]{0,1:T(8,128)}, u32[]{:S(2)}, u32[]{:S(2)}) collective-permute-start(f32[2048,172]{0,1:T(8,128)S(1)} %copy.105), channel_id=1, source_target_pairs={{0,4},{4,8},{8,12},{12,16},{16,20},{20,24},{24,28},{28,0},{1,5},{5... | collective-permute-start | bytes 4227080 | tf_op jit(solution)/shard_map/ppermute | solution.py:17
  466.0 7.1 %copy-start.6 = (f32[172,172]{1,0:T(8,128)S(1)}, f32[172,172]{1,0:T(8,128)}, u32[]{:S(2)}) copy-start(f32[172,172]{1,0:T(8,128)} %get-tuple-element.51) | copy-start | bytes 355012
  466.0 7.1 %copy-start.7 = (f32[172,172]{1,0:T(8,128)S(1)}, f32[172,172]{1,0:T(8,128)}, u32[]{:S(2)}) copy-start(f32[172,172]{1,0:T(8,128)} %get-tuple-element.52) | copy-start | bytes 355012
  466.0 7.1 %copy-start.8 = (f32[172,172]{1,0:T(8,128)S(1)}, f32[172,172]{1,0:T(8,128)}, u32[]{:S(2)}) copy-start(f32[172,172]{1,0:T(8,128)} %get-tuple-element.53) | copy-start | bytes 355012
Sparse Core Ops, SparseCore 0:
  109.8 149.6 all-reduce.20
  314.4 145.7 all-reduce.22
